TPU v7x, 32 devices: a whole 2x2x4 slice. The times are simulated.
32 devices in a mesh: lat: 8 (over z, x), lev: 4 (over y, core).
Axes of the slice: x: 2, y: 2, z: 4, core: 2. Of those that a mesh axis runs over, the one named last changes fastest.
Arguments:
- right_side: float32 [8, 64, 2048], P('lev', 'lat'), may hold values from -6 to 6
- diag_shift: float32 [8, 64, 2048], P('lev', 'lat'), may hold values from 0.5 to 2
- level_scale: float32 [8], P('lev'), may hold values from 0.1 to 1
Outputs:
- solution: float32 [8, 64, 2048], P('lev', 'lat')
- residual: float32 [8, 64, 2048], P('lev', 'lat')
All inputs are finite; a program needn't handle non-finite values.
Results may differ from a plain program's by a relative error of at most 0.0003.
Values sent between devices are 32-bit elements; how exact they have to be, the bound alone decides.
A program may use at most 64 MiB of HBM per device.

v0:
```python
import jax
import jax.numpy as jnp
from jax import lax
from jax.sharding import PartitionSpec as P

WAVES = 640
ITERS = 3


def with_halo(block, sides, width):
    for axis, dim in sides:
        count = lax.axis_size(axis)
        forward = [(i, i + 1) for i in range(count - 1)]
        backward = [(target, source) for source, target in forward]
        low = lax.ppermute(
            lax.slice_in_dim(block, block.shape[dim] - width, None, axis=dim), axis, forward
        )
        high = lax.ppermute(lax.slice_in_dim(block, 0, width, axis=dim), axis, backward)
        block = jnp.concatenate([low, block, high], axis=dim)
    return block


def polar_gain(total_rows, start, count):
    latitude = (start + jnp.arange(count, dtype=jnp.int32)).astype(jnp.float32)
    colatitude = jnp.pi * (4.0 * latitude + 3.0) / (4.0 * total_rows + 2.0)
    return 1.0 / jnp.maximum(jnp.sin(colatitude), 0.5) ** 2


def fourier_table(longitudes, wavenumber, cosine_part):
    position = jnp.arange(longitudes, dtype=jnp.int32)
    product = position[:, None] * wavenumber[None, :] % longitudes
    radians = 2.0 * jnp.pi / longitudes * product.astype(jnp.float32)
    return jnp.where(cosine_part[None, :], jnp.cos(radians), jnp.sin(radians))


def sine_table(latitudes):
    counter = jnp.arange(1, latitudes + 1, dtype=jnp.int32)
    product = counter[:, None] * counter[None, :] % (2 * latitudes + 2)
    return jnp.sin(jnp.pi / (latitudes + 1) * product.astype(jnp.float32))


def spectral_weights(latitudes, longitudes, wavenumber):
    counter = jnp.arange(1, latitudes + 1, dtype=jnp.int32).astype(jnp.float32)
    zonal_part = 4.0 * jnp.sin(jnp.pi / longitudes * wavenumber.astype(jnp.float32)) ** 2
    merid_part = 4.0 * jnp.sin(0.5 * jnp.pi / (latitudes + 1) * counter) ** 2
    scaling = 2.0 / (longitudes * (latitudes + 1))
    return scaling / (1.0 + merid_part[:, None] + zonal_part[None, :])


def stencil(padded, diagonal, level_scale, zonal_gain):
    centre = padded[:, 1:-1, :]
    meridional = padded[:, :-2, :] + padded[:, 2:, :]
    zonal_pair = jnp.roll(centre, 1, axis=2) + jnp.roll(centre, -1, axis=2)
    corners = jnp.roll(meridional, 1, axis=2) + jnp.roll(meridional, -1, axis=2)
    coupling = zonal_gain[None, :, None] * zonal_pair + meridional + 0.125 * corners
    return diagonal * centre - level_scale[:, None, None] * coupling


def operate(field, diagonal, level_scale, zonal_gain):
    padded = with_halo(field, (("lat", 1),), 1)
    midway = field.shape[2] // 2
    position = lax.axis_index("lat")
    final_band = lax.axis_size("lat") - 1
    northern = jnp.roll(field[:, :1, :], midway, axis=2)
    southern = jnp.roll(field[:, -1:, :], midway, axis=2)
    upper_row = jnp.where(position == 0, northern, padded[:, :1, :])
    lower_row = jnp.where(position == final_band, southern, padded[:, -1:, :])
    padded = jnp.concatenate([upper_row, padded[:, 1:-1, :], lower_row], axis=1)
    return stencil(padded, diagonal, level_scale, zonal_gain)


def precondition(current, diagonal, fourier, sines, spectral):
    highest = lax.Precision.HIGHEST
    levels, band_rows, longitudes = current.shape
    columns = fourier.shape[1]
    flattened = current.reshape(levels * band_rows, longitudes)
    coefficients = jnp.dot(
        flattened, fourier, precision=highest, preferred_element_type=jnp.float32
    )
    coefficients = coefficients.reshape(levels, band_rows, columns)

    def meridional(received):
        modes = jnp.einsum("kjc,jl->klc", received, sines, precision=highest) * spectral[None]
        returned = jnp.einsum("klc,jl->kjc", modes, sines, precision=highest)
        return lax.all_to_all(returned, "lat", split_axis=1, concat_axis=2, tiled=True)

    arrived = meridional(
        lax.all_to_all(coefficients, "lat", split_axis=2, concat_axis=1, tiled=True)
    )
    synthesis = lax.dot_general(
        arrived.reshape(levels * band_rows, columns),
        fourier,
        (((1,), (1,)), ((), ())),
        precision=highest,
        preferred_element_type=jnp.float32,
    )
    return 0.5 * current / diagonal + synthesis.reshape(levels, band_rows, longitudes)


def paired_products(residual, adjusted, applied):
    return lax.psum((jnp.sum(residual * adjusted), jnp.sum(applied * adjusted)), ("lat", "lev"))


def body(right_side, diag_shift, level_scale):
    levels, band_rows, longitudes = right_side.shape
    bands = lax.axis_size("lat")
    latitudes = band_rows * bands
    position = lax.axis_index("lat")
    zonal_gain = polar_gain(latitudes, position * band_rows, band_rows)
    diagonal = diag_shift + level_scale[:, None, None] * (2.0 * zonal_gain[None, :, None] + 2.5)
    per_device = WAVES // bands
    columns = jnp.arange(2 * WAVES, dtype=jnp.int32)
    remainder = columns % (2 * per_device)
    wavenumber = columns // (2 * per_device) * per_device + remainder % per_device
    fourier = fourier_table(longitudes, wavenumber, remainder < per_device)
    sines = sine_table(latitudes)
    local_columns = jnp.arange(2 * per_device, dtype=jnp.int32)
    local_waves = position * per_device + local_columns % per_device
    spectral = spectral_weights(latitudes, longitudes, local_waves)

    def apply_operator(field):
        return operate(field, diagonal, level_scale, zonal_gain)

    def apply_inverse(current):
        return precondition(current, diagonal, fourier, sines, spectral)

    solution = jnp.zeros_like(right_side)
    residual = right_side
    adjusted = apply_inverse(residual)
    applied = apply_operator(adjusted)
    aligned, curvature = paired_products(residual, adjusted, applied)
    step_size = aligned / curvature
    direction, image = (adjusted, applied)
    for iteration in range(ITERS):
        solution = solution + step_size * direction
        residual = residual - step_size * image
        if iteration + 1 < ITERS:
            adjusted = apply_inverse(residual)
            applied = apply_operator(adjusted)
            aligned_next, curvature = paired_products(residual, adjusted, applied)
            beta_ratio = aligned_next / aligned
            step_size = aligned_next / (curvature - beta_ratio * aligned_next / step_size)
            direction = adjusted + beta_ratio * direction
            image = applied + beta_ratio * image
            aligned = aligned_next
    return (solution, residual)


def solution(mesh):
    placed = (P("lev", "lat", None), P("lev", "lat", None), P("lev"))
    return jax.shard_map(
        body,
        mesh=mesh,
        in_specs=placed,
        out_specs=(P("lev", "lat", None), P("lev", "lat", None)),
        check_vma=False,
    )
```

profile of v0, /device:TPU:0, one launch (start us, length us, event | category | flops | bytes accessed | tf_op | source)
XLA Modules:
  0.0 550.7 jit_solution(15155512000663679863)
XLA Ops:
  0.7 47.8 %fusion.17 = f32[2,8,1280]{2,1,0:T(8,128)S(1)} fusion(s32[1280]{0:T(1024)S(1)} %fusion.99, pred[1280]{0:T(1024)(128)(4,1)S(1)} %fusion.104, f32[2,8,2048]{2,1,0:T(8,128)} %param.3), kind=kOutput, calls=%fused_computation.21 | convolution fusion | flops 542638080 | bytes 219392 | tf_op jit(solution)/shard_map/dot_general | solution.py:77
  48.5 0.6 copy.36
  49.1 2.8 reshape.181
  51.9 7.6 %all-to-all-start = ((f32[8,1,2560]{2,1,0:T(1,128)}), f32[8,1,2560]{2,1,0:T(1,128)S(1)}, u32[]{:S(2)}, u32[]{:S(2)}) async-start(f32[8,1,2560]{2,1,0:T(1,128)} %reshape.181), calls=%async_computation | async-start | bytes 163840 | tf_op jit(solution)/shard_map/all_to_all | solution.py:88
  59.7 6.7 %all-to-all-done = f32[8,1,2560]{2,1,0:T(1,128)S(1)} async-done(((f32[8,1,2560]{2,1,0:T(1,128)}), f32[8,1,2560]{2,1,0:T(1,128)S(1)}, u32[]{:S(2)}, u32[]{:S(2)}) %all-to-all-start) | async-done | bytes 81952 | tf_op jit(solution)/shard_map/all_to_all | solution.py:88
  66.9 0.8 reduce
  67.8 2.0 reshape.182
  69.8 0.7 copy.59
  71.5 0.8 copy.40
  72.3 3.4 all-to-all-start.1
  75.8 7.1 %all-to-all-done.1 = f32[2,64,160]{2,0,1:T(2,128)S(1)} async-done(((f32[2,64,160]{2,0,1:T(2,128)}), f32[2,64,160]{2,0,1:T(2,128)S(1)}, u32[]{:S(2)}, u32[]{:S(2)}) %all-to-all-start.1) | async-done | bytes 81952 | tf_op jit(solution)/shard_map/all_to_all | solution.py:85
  83.1 50.1 %fusion.18 = f32[2,8,2048]{2,1,0:T(8,128)S(1)} fusion(f32[2,8,1280]{2,1,0:T(8,128)S(1)} %dot_general.48, s32[1280]{0:T(1024)S(1)} %fusion.99, pred[1280]{0:T(1024)(128)(4,1)S(1)} %fusion.104, f32[2,8,2048]{2,1,0:T(8,128)S(1)} %copy-done.1, f32[2,8,2048]{2,1,0:T(8,128)S(1)} %copy-done, f32[2,8]{1,0:T(2,128)S(1)} %broadcast_multiply_fusion), kind=kOutput, calls=%fused_computation.22 | convolution fusion | flops 542769152 | bytes 481600 | tf_op jit(solution)/shard_map/dot_general | solution.py:90
  133.4 2.1 collective-permute-start
  135.6 1.3 collective-permute-start.1
  136.9 4.2 collective-permute-done.1
  141.4 0.8 multiply_reduce_fusion.4
  142.2 49.2 %all-reduce.2 = (f32[]{:T(128)}, f32[]{:T(128)}) all-reduce(f32[]{:T(128)} %get-tuple-element.7, f32[]{:T(128)} %get-tuple-element.6), channel_id=1, replica_groups=mesh['lat'=8,'lev'=4] {'lat','lev'}, use_global_device_ids=true, to_apply=%region_1.2 | all-reduce | flops 2 | bytes 16 | tf_op jit(solution)/shard_map/psum | solution.py:101
  192.8 46.1 %fusion.9 = f32[2,8,1280]{2,1,0:T(8,128)S(1)} fusion(f32[2,8,2048]{2,1,0:T(8,128)S(1)} %multiply_subtract_fusion.2, s32[1280]{0:T(1024)S(1)} %fusion.99, pred[1280]{0:T(1024)(128)(4,1)S(1)} %fusion.104), kind=kOutput, calls=%fused_computation.12 | convolution fusion | flops 542638080 | bytes 219392 | tf_op jit(solution)/shard_map/dot_general | solution.py:77
  238.9 0.6 copy.42
  239.6 2.1 reshape.183
  241.7 11.4 %all_to_all.99 = f32[8,1,2560]{2,1,0:T(1,128)S(1)} all-to-all(f32[8,1,2560]{2,1,0:T(1,128)S(1)} %reshape.183), channel_id=1, replica_groups=mesh['lat'=8,'lev'=4] {'lat'}, dimensions={0} | all-to-all | bytes 163840 | tf_op jit(solution)/shard_map/all_to_all | solution.py:88
  253.1 0.8 reduce.1
  254.0 2.0 reshape.184
  256.0 0.7 copy.62
  256.7 0.5 fusion.28
  257.8 9.7 %all_to_all.100 = f32[2,64,160]{2,0,1:T(2,128)S(1)} all-to-all(f32[2,64,160]{2,0,1:T(2,128)S(1)} %copy.46), channel_id=1, replica_groups=mesh['lat'=8,'lev'=4] {'lat'}, dimensions={1} | all-to-all | bytes 163840 | tf_op jit(solution)/shard_map/all_to_all | solution.py:85
  267.7 50.1 %fusion.21 = f32[2,8,2048]{2,1,0:T(8,128)S(1)} fusion(f32[2,8,1280]{2,1,0:T(8,128)S(1)} %dot_general.53, s32[1280]{0:T(1024)S(1)} %fusion.99, pred[1280]{0:T(1024)(128)(4,1)S(1)} %fusion.104, f32[2,8,2048]{2,1,0:T(8,128)S(1)} %multiply_subtract_fusion.2, f32[2,8,2048]{2,1,0:T(8,128)S(1)} %copy-done, f32[2,8]{1,0:T(2,128)S(1)} %broadcast_multiply_fusion), kind=kOutput, calls=%fused_computation.23 | convolution fusion | flops 542769152 | bytes 481600 | tf_op jit(solution)/shard_map/dot_general | solution.py:90
  317.9 2.1 collective-permute-start.2
  320.1 1.3 collective-permute-start.3
  321.5 4.2 collective-permute-done.3
  326.0 0.9 multiply_reduce_fusion.2
  326.9 40.1 %all-reduce.1 = (f32[]{:T(128)}, f32[]{:T(128)}) all-reduce(f32[]{:T(128)} %get-tuple-element.5, f32[]{:T(128)} %get-tuple-element.4), channel_id=1, replica_groups=mesh['lat'=8,'lev'=4] {'lat','lev'}, use_global_device_ids=true, to_apply=%region_5.6 | all-reduce | flops 2 | bytes 16 | tf_op jit(solution)/shard_map/psum | solution.py:101
  371.4 46.1 %fusion.5 = f32[2,8,1280]{2,1,0:T(8,128)S(1)} fusion(f32[2,8,2048]{2,1,0:T(8,128)S(1)} %multiply_subtract_fusion.1, s32[1280]{0:T(1024)S(1)} %fusion.99, pred[1280]{0:T(1024)(128)(4,1)S(1)} %fusion.104), kind=kOutput, calls=%fused_computation.8 | convolution fusion | flops 542638080 | bytes 219392 | tf_op jit(solution)/shard_map/dot_general | solution.py:77
  417.5 0.6 copy.48
  418.2 2.1 reshape.185
  420.3 11.4 %all_to_all.101 = f32[8,1,2560]{2,1,0:T(1,128)S(1)} all-to-all(f32[8,1,2560]{2,1,0:T(1,128)S(1)} %reshape.185), channel_id=1, replica_groups=mesh['lat'=8,'lev'=4] {'lat'}, dimensions={0} | all-to-all | bytes 163840 | tf_op jit(solution)/shard_map/all_to_all | solution.py:88
  431.7 0.8 reduce.2
  432.6 2.0 reshape.186
  434.6 0.7 copy.65
  435.3 0.5 fusion.27
  436.4 9.7 %all_to_all.102 = f32[2,64,160]{2,0,1:T(2,128)S(1)} all-to-all(f32[2,64,160]{2,0,1:T(2,128)S(1)} %copy.52), channel_id=1, replica_groups=mesh['lat'=8,'lev'=4] {'lat'}, dimensions={1} | all-to-all | bytes 163840 | tf_op jit(solution)/shard_map/all_to_all | solution.py:85
  446.3 50.1 %fusion.24 = f32[2,8,2048]{2,1,0:T(8,128)S(1)} fusion(f32[2,8,1280]{2,1,0:T(8,128)S(1)} %dot_general.58, s32[1280]{0:T(1024)S(1)} %fusion.99, pred[1280]{0:T(1024)(128)(4,1)S(1)} %fusion.104, f32[2,8,2048]{2,1,0:T(8,128)S(1)} %multiply_subtract_fusion.1, f32[2,8,2048]{2,1,0:T(8,128)S(1)} %copy-done, f32[2,8]{1,0:T(2,128)S(1)} %broadcast_multiply_fusion), kind=kOutput, calls=%fused_computation.24 | convolution fusion | flops 542769152 | bytes 481600 | tf_op jit(solution)/shard_map/dot_general | solution.py:90
  496.5 2.1 collective-permute-start.4
  498.7 1.3 collective-permute-start.5
  500.1 4.2 collective-permute-done.5
  504.6 0.8 multiply_reduce_fusion
  505.4 40.3 %all-reduce = (f32[]{:T(128)}, f32[]{:T(128)}) all-reduce(f32[]{:T(128)} %get-tuple-element.3, f32[]{:T(128)} %get-tuple-element.2), channel_id=1, replica_groups=mesh['lat'=8,'lev'=4] {'lat','lev'}, use_global_device_ids=true, to_apply=%region_9.10 | all-reduce | flops 2 | bytes 16 | tf_op jit(solution)/shard_map/psum | solution.py:101
  549.6 0.8 multiply_subtract_fusion
  (60 shorter events, 5.2 us)
Async XLA Ops:
  51.9 14.5 %all-to-all-start = ((f32[8,1,2560]{2,1,0:T(1,128)}), f32[8,1,2560]{2,1,0:T(1,128)S(1)}, u32[]{:S(2)}, u32[]{:S(2)}) async-start(f32[8,1,2560]{2,1,0:T(1,128)} %reshape.181), calls=%async_computation | async-start | bytes 163840 | tf_op jit(solution)/shard_map/all_to_all | solution.py:88
  69.8 5.9 %copy-start.2 = (f32[2]{0:T(128)S(1)}, f32[2]{0:T(128)}, u32[]{:S(2)}) copy-start(f32[2]{0:T(128)} %param.5) | copy-start | bytes 28
  69.8 13.3 %copy-start = (f32[2,8,2048]{2,1,0:T(8,128)S(1)}, f32[2,8,2048]{2,1,0:T(8,128)}, u32[]{:S(2)}) copy-start(f32[2,8,2048]{2,1,0:T(8,128)} %param.4) | copy-start | bytes 393220
  69.8 13.3 %copy-start.1 = (f32[2,8,2048]{2,1,0:T(8,128)S(1)}, f32[2,8,2048]{2,1,0:T(8,128)}, u32[]{:S(2)}) copy-start(f32[2,8,2048]{2,1,0:T(8,128)} %param.3) | copy-start | bytes 393220
  72.3 10.7 %all-to-all-start.1 = ((f32[2,64,160]{2,0,1:T(2,128)}), f32[2,64,160]{2,0,1:T(2,128)S(1)}, u32[]{:S(2)}, u32[]{:S(2)}) async-start(f32[2,64,160]{2,0,1:T(2,128)} %copy.40), calls=%async_computation.1 | async-start | bytes 262144 | tf_op jit(solution)/shard_map/all_to_all | solution.py:85
  133.4 3.6 collective-permute-start
  135.6 5.6 %collective-permute-start.1 = (f32[2,1,2048]{2,1,0:T(1,128)S(1)}, f32[2,1,2048]{2,1,0:T(1,128)S(1)}, u32[]{:S(2)}, u32[]{:S(2)}) collective-permute-start(f32[2,1,2048]{2,1,0:T(1,128)S(1)} %get-tuple-element.58), channel_id=1, source_target_pairs={{4,0},{8,4},{12,8},{16,12},{20,16},{24,20},{28,24},{5,1},{9,5},{13... | collective-permute-start | bytes 49160 | tf_op jit(solution)/shard_map/ppermute | solution.py:18
  317.9 3.6 collective-permute-start.2
  320.1 5.6 %collective-permute-start.3 = (f32[2,1,2048]{2,1,0:T(1,128)S(1)}, f32[2,1,2048]{2,1,0:T(1,128)S(1)}, u32[]{:S(2)}, u32[]{:S(2)}) collective-permute-start(f32[2,1,2048]{2,1,0:T(1,128)S(1)} %get-tuple-element.44), channel_id=1, source_target_pairs={{4,0},{8,4},{12,8},{16,12},{20,16},{24,20},{28,24},{5,1},{9,5},{13... | collective-permute-start | bytes 49160 | tf_op jit(solution)/shard_map/ppermute | solution.py:18
  496.5 3.6 collective-permute-start.4
  498.7 5.6 %collective-permute-start.5 = (f32[2,1,2048]{2,1,0:T(1,128)S(1)}, f32[2,1,2048]{2,1,0:T(1,128)S(1)}, u32[]{:S(2)}, u32[]{:S(2)}) collective-permute-start(f32[2,1,2048]{2,1,0:T(1,128)S(1)} %get-tuple-element.30), channel_id=1, source_target_pairs={{4,0},{8,4},{12,8},{16,12},{20,16},{24,20},{28,24},{5,1},{9,5},{13... | collective-permute-start | bytes 49160 | tf_op jit(solution)/shard_map/ppermute | solution.py:18
where the time goes:
time: 560 us; the launch traced here: 551 us
  matrix products  293 us (52%)
  blocking collectives  172 us (31%)
  waiting for transfers between devices  26.8 us (5%)
  starting transfers between devices  21.1 us (4%)
  local copies, waits for them, and re-layouts  20.1 us (4%)
  between operations  11.2 us (2%)
  other arithmetic  6.44 us (1%)
    dot_general x3, matrix products, precondition(): lax.dot_general(arrived.reshape(levels * band_rows, columns), fourier, ((...  150 us
    dot_general x3, matrix products, precondition(): jnp.dot(flattened, fourier, precision=highest, preferred_element_type=jnp...  140 us
    psum x3, blocking collectives, paired_products(): lax.psum((jnp.sum(residual * adjusted), jnp.sum(applied * adjusted)), ('l...  130 us
    all_to_all x2, blocking collectives, precondition(): lax.all_to_all(coefficients, 'lat', split_axis=2, concat_axis=1, tiled=True)  22.9 us
    all_to_all x2, blocking collectives, meridional(): lax.all_to_all(returned, 'lat', split_axis=1, concat_axis=2, tiled=True)  19.5 us
    unnamed x12, local copies, waits for them, and re-layouts  13 us
    ppermute x3, waiting for transfers between devices, with_halo(): lax.ppermute(lax.slice_in_dim(block, 0, width, axis=dim), axis, backward)  12.7 us
  transfers between devices with their start and end apart: 8, of which 8 were waited for; matrix products, arithmetic and copies ran while one was open for 0% of the time, Pallas kernels for 0%

commit v1 on v0

--- a/solution.py
+++ b/solution.py
@@ -5,6 +5,15 @@
 
 WAVES = 640
 ITERS = 3
+
+
+def column_mix(in_array, shard_axis):
+    return jnp.concatenate(
+        lax.all_to_all(
+            jnp.stack(jnp.split(in_array, lax.axis_size(shard_axis), 2), 0), shard_axis, 0, 0
+        ),
+        1,
+    )
 
 
 def with_halo(block, sides, width):
@@ -84,9 +93,7 @@
         returned = jnp.einsum("klc,jl->kjc", modes, sines, precision=highest)
         return lax.all_to_all(returned, "lat", split_axis=1, concat_axis=2, tiled=True)
 
-    arrived = meridional(
-        lax.all_to_all(coefficients, "lat", split_axis=2, concat_axis=1, tiled=True)
-    )
+    arrived = meridional(column_mix(coefficients, "lat"))
     synthesis = lax.dot_general(
         arrived.reshape(levels * band_rows, columns),
         fourier,

time: 560 us -> 540 us (0.964)
  local copies, waits for them, and re-layouts: 20.1 us -> 9.62 us
  blocking collectives: 172 us -> 165 us
    psum x3, blocking collectives: 130 us -> 121 us  [paired_products(): lax.psum((jnp.sum(residual * adjusted), jnp.sum(applied * adjusted)), ('l...]
    unnamed x12 -> x27, local copies, waits for them, and re-layouts: 13 us -> 6.16 us
where the time goes in v1:
time: 540 us; the launch traced here: 531 us
  matrix products  293 us (54%)
  blocking collectives  165 us (31%)
  waiting for transfers between devices  27.1 us (5%)
  starting transfers between devices  21.2 us (4%)
  between operations  10.9 us (2%)
  local copies, waits for them, and re-layouts  9.62 us (2%)
    dot_general x3, matrix products, precondition(): lax.dot_general(arrived.reshape(levels * band_rows, columns), fourier, ((...  150 us
    dot_general x3, matrix products, precondition(): jnp.dot(flattened, fourier, precision=highest, preferred_element_type=jnp...  140 us
    psum x3, blocking collectives, paired_products(): lax.psum((jnp.sum(residual * adjusted), jnp.sum(applied * adjusted)), ('l...  121 us
    all_to_all x2, blocking collectives, column_mix(): lax.all_to_all(jnp.stack(jnp.split(in_array, lax.axis_size(shard_axis), 2...  23.5 us
    all_to_all x2, blocking collectives, meridional(): lax.all_to_all(returned, 'lat', split_axis=1, concat_axis=2, tiled=True)  19.9 us
    ppermute x3, waiting for transfers between devices, with_halo(): lax.ppermute(lax.slice_in_dim(block, 0, width, axis=dim), axis, backward)  12.7 us
  transfers between devices with their start and end apart: 8, of which 8 were waited for; matrix products, arithmetic and copies ran while one was open for 0% of the time, Pallas kernels for 0%

profile of v1, /device:TPU:0, one launch (start us, length us, event | category | flops | bytes accessed | tf_op | source)
XLA Modules:
  0.0 530.7 jit_solution(12528083210708488351)
XLA Ops:
  0.7 47.8 %fusion.17 = f32[2,8,1280]{2,1,0:T(8,128)S(1)} fusion(s32[1280]{0:T(1024)S(1)} %fusion.102, pred[1280]{0:T(1024)(128)(4,1)S(1)} %fusion.107, f32[2,8,2048]{2,1,0:T(8,128)} %param.3), kind=kOutput, calls=%fused_computation.21 | convolution fusion | flops 542638080 | bytes 219392 | tf_op jit(solution)/shard_map/dot_general | solution.py:86
  48.5 0.6 constant_dynamic-update-slice_fusion.7
  49.1 0.7 constant_dynamic-update-slice_fusion.6
  49.8 0.7 constant_dynamic-update-slice_fusion.5
  50.5 0.7 constant_dynamic-update-slice_fusion.4
  51.1 0.6 constant_dynamic-update-slice_fusion.3
  51.7 0.7 constant_dynamic-update-slice_fusion.2
  52.4 0.7 constant_dynamic-update-slice_fusion.1
  53.1 0.7 constant_dynamic-update-slice_fusion
  53.8 7.3 %all-to-all-start = ((f32[8,2,8,160]{3,2,1,0:T(8,128)}), f32[8,2,8,160]{3,2,1,0:T(8,128)S(1)}, u32[]{:S(2)}, u32[]{:S(2)}) async-start(f32[8,2,8,160]{3,2,1,0:T(8,128)} %constant_dynamic-update-slice_fusion), calls=%async_computation | async-start | bytes 262144 | tf_op jit(solution)/shard_map/all_to_all | solution.py:12
  61.3 7.1 %all-to-all-done = f32[8,2,8,160]{3,2,1,0:T(8,128)S(1)} async-done(((f32[8,2,8,160]{3,2,1,0:T(8,128)}), f32[8,2,8,160]{3,2,1,0:T(8,128)S(1)}, u32[]{:S(2)}, u32[]{:S(2)}) %all-to-all-start) | async-done | bytes 81952 | tf_op jit(solution)/shard_map/all_to_all | solution.py:12
  68.4 0.5 fusion.29
  68.9 0.4 convolution_bitcast_fusion.2
  69.4 0.8 copy.22
  70.1 3.7 all-to-all-start.1
  74.0 7.1 %all-to-all-done.1 = f32[2,64,160]{2,0,1:T(2,128)S(1)} async-done(((f32[2,64,160]{2,0,1:T(2,128)}), f32[2,64,160]{2,0,1:T(2,128)S(1)}, u32[]{:S(2)}, u32[]{:S(2)}) %all-to-all-start.1) | async-done | bytes 81952 | tf_op jit(solution)/shard_map/all_to_all | solution.py:94
  81.2 0.1 dot_general.48
  81.3 0.7 copy-done.1
  82.1 50.0 %fusion.18 = f32[2,8,2048]{2,1,0:T(8,128)S(1)} fusion(f32[2,8,1280]{2,1,0:T(8,128)S(1)} %dot_general.48, s32[1280]{0:T(1024)S(1)} %fusion.102, pred[1280]{0:T(1024)(128)(4,1)S(1)} %fusion.107, f32[2,8,2048]{2,1,0:T(8,128)S(1)} %copy-done.1, f32[2,8,2048]{2,1,0:T(8,128)S(1)} %copy-done, f32[2,8]{1,0:T(2,128)S(1)} %broadcast_multiply_fusion), kind=kOutput, calls=%fused_computation.22 | convolution fusion | flops 542769152 | bytes 481600 | tf_op jit(solution)/shard_map/dot_general | solution.py:97
  132.4 2.1 collective-permute-start
  134.6 1.3 collective-permute-start.1
  135.9 4.2 collective-permute-done.1
  140.4 0.8 multiply_reduce_fusion.4
  141.2 40.9 %all-reduce.2 = (f32[]{:T(128)}, f32[]{:T(128)}) all-reduce(f32[]{:T(128)} %get-tuple-element.7, f32[]{:T(128)} %get-tuple-element.6), channel_id=1, replica_groups=mesh['lat'=8,'lev'=4] {'lat','lev'}, use_global_device_ids=true, to_apply=%region_1.2 | all-reduce | flops 2 | bytes 16 | tf_op jit(solution)/shard_map/psum | solution.py:108
  183.5 46.1 %fusion.9 = f32[2,8,1280]{2,1,0:T(8,128)S(1)} fusion(f32[2,8,2048]{2,1,0:T(8,128)S(1)} %multiply_subtract_fusion.2, s32[1280]{0:T(1024)S(1)} %fusion.102, pred[1280]{0:T(1024)(128)(4,1)S(1)} %fusion.107), kind=kOutput, calls=%fused_computation.12 | convolution fusion | flops 542638080 | bytes 219392 | tf_op jit(solution)/shard_map/dot_general | solution.py:86
  230.1 11.8 %all_to_all.60 = f32[8,2,8,160]{3,2,1,0:T(8,128)S(1)} all-to-all(f32[8,2,8,160]{3,2,1,0:T(8,128)S(1)} %constant_dynamic-update-slice_fusion.8), channel_id=1, replica_groups=mesh['lat'=8,'lev'=4] {'lat'}, dimensions={0} | all-to-all | bytes 163840 | tf_op jit(solution)/shard_map/all_to_all | solution.py:12
  241.8 0.5 fusion.28
  242.3 0.5 convolution_bitcast_fusion.1
  242.9 9.9 %all_to_all.61 = f32[2,64,160]{2,0,1:T(2,128)S(1)} all-to-all(f32[2,64,160]{2,0,1:T(2,128)S(1)} %copy.26), channel_id=1, replica_groups=mesh['lat'=8,'lev'=4] {'lat'}, dimensions={1} | all-to-all | bytes 163840 | tf_op jit(solution)/shard_map/all_to_all | solution.py:94
  252.9 0.1 dot_general.53
  253.0 50.1 %fusion.21 = f32[2,8,2048]{2,1,0:T(8,128)S(1)} fusion(f32[2,8,1280]{2,1,0:T(8,128)S(1)} %dot_general.53, s32[1280]{0:T(1024)S(1)} %fusion.102, pred[1280]{0:T(1024)(128)(4,1)S(1)} %fusion.107, f32[2,8,2048]{2,1,0:T(8,128)S(1)} %multiply_subtract_fusion.2, f32[2,8,2048]{2,1,0:T(8,128)S(1)} %copy-done, f32[2,8]{1,0:T(2,128)S(1)} %broadcast_multiply_fusion), kind=kOutput, calls=%fused_computation.23 | convolution fusion | flops 542769152 | bytes 481600 | tf_op jit(solution)/shard_map/dot_general | solution.py:97
  303.2 2.1 collective-permute-start.2
  305.4 1.3 collective-permute-start.3
  306.8 4.2 collective-permute-done.3
  311.3 0.8 multiply_reduce_fusion.2
  312.2 39.9 %all-reduce.1 = (f32[]{:T(128)}, f32[]{:T(128)}) all-reduce(f32[]{:T(128)} %get-tuple-element.5, f32[]{:T(128)} %get-tuple-element.4), channel_id=1, replica_groups=mesh['lat'=8,'lev'=4] {'lat','lev'}, use_global_device_ids=true, to_apply=%region_5.6 | all-reduce | flops 2 | bytes 16 | tf_op jit(solution)/shard_map/psum | solution.py:108
  356.5 46.1 %fusion.5 = f32[2,8,1280]{2,1,0:T(8,128)S(1)} fusion(f32[2,8,2048]{2,1,0:T(8,128)S(1)} %multiply_subtract_fusion.1, s32[1280]{0:T(1024)S(1)} %fusion.102, pred[1280]{0:T(1024)(128)(4,1)S(1)} %fusion.107), kind=kOutput, calls=%fused_computation.8 | convolution fusion | flops 542638080 | bytes 219392 | tf_op jit(solution)/shard_map/dot_general | solution.py:86
  403.0 11.8 %all_to_all.62 = f32[8,2,8,160]{3,2,1,0:T(8,128)S(1)} all-to-all(f32[8,2,8,160]{3,2,1,0:T(8,128)S(1)} %constant_dynamic-update-slice_fusion.16), channel_id=1, replica_groups=mesh['lat'=8,'lev'=4] {'lat'}, dimensions={0} | all-to-all | bytes 163840 | tf_op jit(solution)/shard_map/all_to_all | solution.py:12
  414.8 0.5 fusion.27
  415.4 0.5 convolution_bitcast_fusion
  415.9 10.0 %all_to_all.63 = f32[2,64,160]{2,0,1:T(2,128)S(1)} all-to-all(f32[2,64,160]{2,0,1:T(2,128)S(1)} %copy.30), channel_id=1, replica_groups=mesh['lat'=8,'lev'=4] {'lat'}, dimensions={1} | all-to-all | bytes 163840 | tf_op jit(solution)/shard_map/all_to_all | solution.py:94
  426.1 50.1 %fusion.24 = f32[2,8,2048]{2,1,0:T(8,128)S(1)} fusion(f32[2,8,1280]{2,1,0:T(8,128)S(1)} %dot_general.58, s32[1280]{0:T(1024)S(1)} %fusion.102, pred[1280]{0:T(1024)(128)(4,1)S(1)} %fusion.107, f32[2,8,2048]{2,1,0:T(8,128)S(1)} %multiply_subtract_fusion.1, f32[2,8,2048]{2,1,0:T(8,128)S(1)} %copy-done, f32[2,8]{1,0:T(2,128)S(1)} %broadcast_multiply_fusion), kind=kOutput, calls=%fused_computation.24 | convolution fusion | flops 542769152 | bytes 481600 | tf_op jit(solution)/shard_map/dot_general | solution.py:97
  476.3 2.1 collective-permute-start.4
  478.5 1.3 collective-permute-start.5
  479.9 4.2 collective-permute-done.5
  484.4 0.8 multiply_reduce_fusion
  485.2 40.5 %all-reduce = (f32[]{:T(128)}, f32[]{:T(128)}) all-reduce(f32[]{:T(128)} %get-tuple-element.3, f32[]{:T(128)} %get-tuple-element.2), channel_id=1, replica_groups=mesh['lat'=8,'lev'=4] {'lat','lev'}, use_global_device_ids=true, to_apply=%region_9.10 | all-reduce | flops 2 | bytes 16 | tf_op jit(solution)/shard_map/psum | solution.py:108
  529.5 0.8 multiply_subtract_fusion
  (68 shorter events, 3.6 us)
Async XLA Ops:
  53.8 14.6 %all-to-all-start = ((f32[8,2,8,160]{3,2,1,0:T(8,128)}), f32[8,2,8,160]{3,2,1,0:T(8,128)S(1)}, u32[]{:S(2)}, u32[]{:S(2)}) async-start(f32[8,2,8,160]{3,2,1,0:T(8,128)} %constant_dynamic-update-slice_fusion), calls=%async_computation | async-start | bytes 262144 | tf_op jit(solution)/shard_map/all_to_all | solution.py:12
  70.1 3.7 copy-start.2
  70.1 11.0 %all-to-all-start.1 = ((f32[2,64,160]{2,0,1:T(2,128)}), f32[2,64,160]{2,0,1:T(2,128)S(1)}, u32[]{:S(2)}, u32[]{:S(2)}) async-start(f32[2,64,160]{2,0,1:T(2,128)} %copy.22), calls=%async_computation.1 | async-start | bytes 262144 | tf_op jit(solution)/shard_map/all_to_all | solution.py:94
  81.1 0.9 copy-start.1
  81.2 0.9 copy-start
  132.4 3.6 collective-permute-start
  134.6 5.6 %collective-permute-start.1 = (f32[2,1,2048]{2,1,0:T(1,128)S(1)}, f32[2,1,2048]{2,1,0:T(1,128)S(1)}, u32[]{:S(2)}, u32[]{:S(2)}) collective-permute-start(f32[2,1,2048]{2,1,0:T(1,128)S(1)} %get-tuple-element.58), channel_id=1, source_target_pairs={{4,0},{8,4},{12,8},{16,12},{20,16},{24,20},{28,24},{5,1},{9,5},{13... | collective-permute-start | bytes 49160 | tf_op jit(solution)/shard_map/ppermute | solution.py:27
  303.2 3.6 collective-permute-start.2
  305.4 5.6 %collective-permute-start.3 = (f32[2,1,2048]{2,1,0:T(1,128)S(1)}, f32[2,1,2048]{2,1,0:T(1,128)S(1)}, u32[]{:S(2)}, u32[]{:S(2)}) collective-permute-start(f32[2,1,2048]{2,1,0:T(1,128)S(1)} %get-tuple-element.44), channel_id=1, source_target_pairs={{4,0},{8,4},{12,8},{16,12},{20,16},{24,20},{28,24},{5,1},{9,5},{13... | collective-permute-start | bytes 49160 | tf_op jit(solution)/shard_map/ppermute | solution.py:27
  476.3 3.6 collective-permute-start.4
  478.5 5.6 %collective-permute-start.5 = (f32[2,1,2048]{2,1,0:T(1,128)S(1)}, f32[2,1,2048]{2,1,0:T(1,128)S(1)}, u32[]{:S(2)}, u32[]{:S(2)}) collective-permute-start(f32[2,1,2048]{2,1,0:T(1,128)S(1)} %get-tuple-element.30), channel_id=1, source_target_pairs={{4,0},{8,4},{12,8},{16,12},{20,16},{24,20},{28,24},{5,1},{9,5},{13... | collective-permute-start | bytes 49160 | tf_op jit(solution)/shard_map/ppermute | solution.py:27
